TPU v7x, 128 devices: a whole 4x4x4 slice. The times are simulated.
128 devices in a mesh: mx: 4 (over z), my: 4 (over y_hi, core), col: 8 (over y_lo, x).
Axes of the slice: x: 4, y: 4 (y_hi: 2, y_lo: 2; y = y_hi * 2 + y_lo), z: 4, core: 2. Of those that a mesh axis runs over, the one named last changes fastest.
Arguments:
- spectrum: float32 [2, 16, 128, 32, 512], P(None, 'col', None, 'mx', 'my'), may hold values from -6 to 6
- core_tensor: float32 [2, 64, 64, 16, 16, 16], P(None, 'col', None, ('mx', 'my')), may hold values from -0.01171875 to 0.01171875
- input_factor: float32 [128, 64], replicated, may hold values from -0.5 to 0.5
- output_factor: float32 [128, 64], replicated, may hold values from -0.75 to 0.75
- first_factor: float32 [32, 16], P('mx'), may hold values from -5 to 5
- second_factor: float32 [32, 16], P('my'), may hold values from -5 to 5
- third_factor: float32 [16, 16], replicated, may hold values from -5 to 5
Outputs:
- mixed_modes: float32 [2, 16, 128, 32, 512], P(None, 'col', None, 'mx', 'my')
All inputs are finite; a program needn't handle non-finite values.
Results may differ from a plain program's by a relative error of at most 0.00007.
Values sent between devices are 32-bit elements; how exact they have to be, the bound alone decides.
A program may use at most 128 MiB of HBM per device.

v0:
```python
import jax
import jax.numpy as jnp
from jax import lax
from jax.experimental import pallas as pl
from jax.experimental.pallas import tpu as pltpu
from jax.sharding import PartitionSpec as P

MESH = pl.DeviceIdType.MESH
HIGH = lax.Precision.HIGH
HIGHEST = lax.Precision.HIGHEST
F32 = jnp.float32


def dot(a, b, dims=((1,), (0,)), precision=HIGH):
    return lax.dot_general(a, b, (dims, ((), ())), precision=precision, preferred_element_type=F32)


def iota(shape, dim):
    return lax.broadcasted_iota(jnp.int32, shape, dim)


def kernel(
    spec_hbm, core_hbm, fin_ref, fout_ref, first_ref, second_ref, third_ref,
    out_ref,
    spec, core, xs, xr, bs, br, cs, cr, ys, yr, stage, fr, sr, m1, m2, gout, coef,
    in_sem, fac_send, fac_recv, b_send, b_recv, x_send, x_recv, c_send, c_recv, y_send, y_recv,
):
    z, my, col = lax.axis_index("mx"), lax.axis_index("my"), lax.axis_index("col")
    h, e = my // 2, my % 2
    l, x = col // 4, col % 4
    kz = z * 4 + x

    load_spec = pltpu.make_async_copy(spec_hbm, spec, in_sem.at[0])
    load_core = pltpu.make_async_copy(core_hbm, core, in_sem.at[1])
    load_core.start()
    load_spec.start()

    def plane(i):
        d = i + 1
        return (z + d // 8) % 4, my, ((l + (d // 4) % 2) % 2) * 4 + (x + d % 4) % 4

    def square(i):
        d = i + 1
        return z, ((h + d // 4) % 2) * 2 + (e + d % 2) % 2, ((l + (d // 2) % 2) % 2) * 4 + x

    barrier = pltpu.get_barrier_semaphore()

    def greet_plane(i, carry):
        pl.semaphore_signal(barrier, inc=1, device_id=plane(i), device_id_type=MESH)
        return carry

    def greet_square(i, carry):
        d = i + jnp.where(i >= 1, 1, 0)
        pl.semaphore_signal(barrier, inc=1, device_id=square(d), device_id_type=MESH)
        return carry

    lax.fori_loop(0, 31, greet_plane, 0)
    lax.fori_loop(0, 6, greet_square, 0)

    stage[...] = jnp.zeros_like(stage)
    stage[0, :, 0:16] = first_ref[...]
    stage[1, :, 0:16] = second_ref[...]
    fr[pl.ds(z, 1)] = stage[0:1]
    sr[pl.ds(my, 1)] = stage[1:2]

    spread = jnp.where(iota((16, 256), 1) % 16 == iota((16, 256), 0), 1.0, 0.0)
    wide = dot(third_ref[...], spread, precision=HIGHEST)
    wide = jnp.broadcast_to(wide[:, None, :], (16, 16, 256)).reshape(256, 256)
    m1[...] = jnp.where(iota((256, 256), 0) % 16 == iota((256, 256), 1) // 16, wide, 0.0)

    load_core.wait()

    def third_step(p, carry):
        both = jnp.concatenate([core[0, p], core[1, p]], axis=1)
        bs[:, p] = dot(m1[...], both).reshape(16, 16, 128)
        return carry

    lax.fori_loop(0, 8, third_step, 0)
    pl.semaphore_wait(barrier, 37)

    def send_first(i, carry):
        pltpu.make_async_remote_copy(
            stage.at[0], fr.at[z], fac_send.at[0], fac_recv.at[0],
            device_id=((z + i + 1) % 4, my, col), device_id_type=MESH,
        ).start()
        d = i + 1
        pltpu.make_async_remote_copy(
            stage.at[1], sr.at[my], fac_send.at[1], fac_recv.at[1],
            device_id=(z, ((h + d // 2) % 2) * 2 + (e + d % 2) % 2, col), device_id_type=MESH,
        ).start()
        return carry

    lax.fori_loop(0, 3, send_first, 0)

    def send_b(i, carry):
        d = i + 1
        tz, tx = (z + d // 4) % 4, (x + d % 4) % 4
        pltpu.make_async_remote_copy(
            bs.at[tz * 4 + tx], br.at[z, x], b_send, b_recv,
            device_id=(tz, my, l * 4 + tx), device_id_type=MESH,
        ).start()
        return carry

    lax.fori_loop(0, 15, send_b, 0)
    br[z, x] = bs[kz]

    load_spec.wait()
    xs2 = xs.reshape(2048, 128)

    def project(bk, carry):
        b, k = bk // 8, bk % 8
        real = dot(fin_ref[...], spec[pl.ds(b * 1024 + k, 128, stride=8), :])
        imag = dot(fin_ref[...], spec[pl.ds((2 + b) * 1024 + k, 128, stride=8), :])
        xs2[pl.ds(bk, 128, stride=16), :] = jnp.concatenate([real, imag], axis=0).T
        return carry

    lax.fori_loop(0, 16, project, 0)

    def send_x(i, carry):
        tz, tmy, tcol = plane(i)
        pltpu.make_async_remote_copy(
            xs.at[tcol // 4, :, tz * 4 + tcol % 4], xr.at[:, z * 8 + col], x_send, x_recv,
            device_id=(tz, tmy, tcol), device_id_type=MESH,
        ).start()
        return carry

    lax.fori_loop(0, 31, send_x, 0)
    for j in range(4):
        xr[j, z * 8 + col] = xs[l, j, kz]

    pltpu.make_async_copy(sr.at[0:3], sr.at[0:3], fac_recv.at[1]).wait()
    spread2 = jnp.where(iota((128, 128), 1) % 16 == iota((128, 128), 0), 1.0, 0.0)
    wide2 = dot(sr[...].reshape(32, 128), spread2, precision=HIGHEST)
    wide2 = jnp.broadcast_to(wide2[:, None, :], (32, 8, 128)).reshape(256, 128)
    m2[...] = jnp.where(iota((256, 128), 0) % 8 == iota((256, 128), 1) // 16, wide2, 0.0)

    pltpu.make_async_copy(bs.at[0:15], bs.at[0:15], b_recv).wait()

    def second_step(i, carry):
        zs, xsrc = i // 4, i % 4
        block = br[zs, xsrc].reshape(128, 128)
        cs[:, :, zs, pl.ds(xsrc * 8, 8), :] = dot(m2[...], block).reshape(8, 4, 8, 128)
        return carry

    lax.fori_loop(0, 16, second_step, 0)

    def send_c(n, carry):
        j, i = n // 7, n % 7
        tz, tmy, tcol = square(i)
        pltpu.make_async_remote_copy(
            cs.at[tmy * 2 + tcol // 4, j], cr.at[j, :, my, pl.ds(l * 32, 32), :],
            c_send, c_recv.at[j],
            device_id=(tz, tmy, tcol), device_id_type=MESH,
        ).start()
        return carry

    lax.fori_loop(0, 28, send_c, 0)

    def keep_c(n, carry):
        j, zs = n // 4, n % 4
        cr[j, zs, my, pl.ds(l * 32, 32), :] = cs[my * 2 + l, j, zs]
        return carry

    lax.fori_loop(0, 16, keep_c, 0)

    gout[...] = jnp.zeros_like(gout)
    turned = fout_ref[...].T
    gout[0:128, 0:64] = turned
    gout[128:256, 64:128] = turned
    pltpu.make_async_copy(sr.at[0:3], sr.at[0:3], fac_recv.at[0]).wait()
    for s in range(16):
        coef[s] = jnp.broadcast_to(fr[...].reshape(32, 128)[:, s : s + 1], (32, 128))
    pltpu.make_async_copy(xr.at[:, 0:31], xr.at[:, 0:31], x_recv).wait()

    sign = jnp.where(iota((64, 128), 1) < 64, -1.0, 1.0)

    def mode_step(j, carry):
        pltpu.make_async_copy(cs.at[0:7, 0], cs.at[0:7, 0], c_recv.at[j]).wait()
        rows = xr[j].reshape(512, 128)

        def group(g, inner):
            parts = []
            for i in range(4):
                top = cr[j, g, i]
                parts.append(jnp.concatenate([top, pltpu.roll(top, 64, 1) * sign], axis=0))
            prod = dot(rows, jnp.concatenate(parts, axis=1))
            total = None
            for i in range(4):
                piece = prod[:, i * 128 : (i + 1) * 128].reshape(4, 16, 8, 128)
                term = piece * coef[g * 4 + i].reshape(4, 1, 8, 128)
                total = term if total is None else total + term
            total = total.reshape(32, 16, 128)

            @pl.when(g == 0)
            def _():
                ys[j] = total

            @pl.when(g > 0)
            def _():
                ys[j] += total

            return inner

        lax.fori_loop(0, 4, group, 0)

        def send_y(i, inner):
            tz, tmy, tcol = plane(i)
            pltpu.make_async_remote_copy(
                ys.at[j, tz * 8 + tcol], yr.at[l, j, kz], y_send, y_recv,
                device_id=(tz, tmy, tcol), device_id_type=MESH,
            ).start()
            return inner

        lax.fori_loop(0, 31, send_y, 0)
        yr[l, j, kz] = ys[j, z * 8 + col]
        return carry

    lax.fori_loop(0, 4, mode_step, 0)
    pltpu.make_async_copy(ys.at[:, 0:31], ys.at[:, 0:31], y_recv).wait()
    yr2 = yr.reshape(2048, 128)

    def finish(bk, carry):
        b, k = bk // 8, bk % 8
        modes = yr2[pl.ds(bk, 128, stride=16), :]
        mixed = dot(gout[...], modes, ((1,), (1,)))
        out_ref[pl.ds(b * 1024 + k, 128, stride=8), :] = mixed[0:128]
        out_ref[pl.ds((2 + b) * 1024 + k, 128, stride=8), :] = mixed[128:256]
        return carry

    lax.fori_loop(0, 16, finish, 0)

    pltpu.make_async_copy(sr.at[0:3], sr.at[0:3], fac_send.at[0]).wait()
    pltpu.make_async_copy(sr.at[0:3], sr.at[0:3], fac_send.at[1]).wait()
    pltpu.make_async_copy(bs.at[0:15], bs.at[0:15], b_send).wait()
    pltpu.make_async_copy(xr.at[:, 0:31], xr.at[:, 0:31], x_send).wait()
    pltpu.make_async_copy(cs.at[0:7], cs.at[0:7], c_send).wait()
    pltpu.make_async_copy(ys.at[:, 0:31], ys.at[:, 0:31], y_send).wait()


def per_device(
    spectrum, core_tensor, input_factor, output_factor, first_factor, second_factor, third_factor
):
    spec = spectrum.reshape(4096, 128)
    core = jnp.transpose(core_tensor[:, :, :, 0], (0, 1, 3, 4, 2)).reshape(2, 8, 256, 64)
    anywhere = pl.BlockSpec(memory_space=pl.ANY)
    near = pl.BlockSpec(memory_space=pltpu.VMEM)
    vmem = lambda *shape: pltpu.VMEM(shape, F32)
    dma = pltpu.SemaphoreType.DMA
    out = pl.pallas_call(
        kernel,
        out_shape=jax.ShapeDtypeStruct((4096, 128), F32),
        in_specs=[anywhere, anywhere] + [near] * 5,
        out_specs=near,
        scratch_shapes=[
            vmem(4096, 128),
            vmem(2, 8, 256, 64),
            vmem(2, 4, 16, 16, 128),
            vmem(4, 32, 16, 128),
            vmem(16, 8, 16, 128),
            vmem(4, 4, 8, 16, 128),
            vmem(8, 4, 4, 32, 128),
            vmem(4, 4, 4, 64, 128),
            vmem(4, 32, 16, 128),
            vmem(2, 4, 16, 16, 128),
            vmem(2, 8, 128),
            vmem(4, 8, 128),
            vmem(4, 8, 128),
            vmem(256, 256),
            vmem(256, 128),
            vmem(256, 128),
            vmem(16, 32, 128),
            dma((2,)), dma((2,)), dma((2,)), dma, dma, dma, dma, dma, dma((4,)), dma, dma,
        ],
        compiler_params=pltpu.CompilerParams(
            collective_id=0, has_side_effects=True, vmem_limit_bytes=60 * 1024 * 1024
        ),
    )(spec, core, input_factor.T, output_factor.T, first_factor, second_factor, third_factor)
    return out.reshape(2, 2, 128, 8, 128)


def solution(mesh):
    placed = (
        P(None, "col", None, "mx", "my"),
        P(None, "col", None, ("mx", "my"), None, None),
        P(),
        P(),
        P("mx", None),
        P("my", None),
        P(),
    )
    return jax.shard_map(
        per_device,
        mesh=mesh,
        in_specs=placed,
        out_specs=P(None, "col", None, "mx", "my"),
        check_vma=False,
    )
```

profile of v0, /device:TPU:1, one launch (start us, length us, event | category | flops | bytes accessed | tf_op | source)
XLA Modules:
  0.0 83.4 jit_solution(17494553583185790341)
XLA Ops:
  0.0 80.3 %shard_map.73 = f32[4096,128]{1,0:T(8,128)} custom-call(f32[4096,128]{1,0:T(8,128)} %bitcast.10, f32[2,8,256,64]{3,2,1,0:T(8,128)} %bitcast.11, f32[64,128]{1,0:T(8,128)} %bitcast.12, f32[64,128]{1,0:T(8,128)} %bitcast.13, f32[8,16]{1,0:T(8,128)} %first_ref.1, f32[8,16]{1,0:T(8,128)} %second_ref.1, f32[16,16]{1,0:T(8,128)} %third_ref.1), custom_call_target="tpu_custom_call" | custom-call | tf_op jit(solution)/shard_map/pallas_call | solution.py:249
  80.4 3.0 %copy.9 = f32[2,2,128,8,128]{4,3,2,1,0:T(8,128)} copy(f32[2,2,128,8,128]{4,3,2,1,0:T(8,128)} %bitcast.9) | data formatting | bytes 4194304
where the time goes:
time: 83.6 us; the launch traced here: 83.4 us
  Pallas kernels  80.3 us (96%)
  local copies, waits for them, and re-layouts  3.05 us (4%)
    pallas_call x1, Pallas kernels, per_device(): pl.pallas_call(kernel, out_shape=jax.ShapeDtypeStruct((4096, 128), F32),...  80.3 us
    unnamed x1, local copies, waits for them, and re-layouts  3.05 us

commit v1 on v0

v1 whole, which is shorter than its diff:
```python
import jax
import jax.numpy as jnp
from jax import lax
from jax.experimental import pallas as pl
from jax.experimental.pallas import tpu as pltpu
from jax.sharding import PartitionSpec as P

MESH = pl.DeviceIdType.MESH
HIGH = lax.Precision.HIGH
HIGHEST = lax.Precision.HIGHEST
F32 = jnp.float32


def dot(a, b, dims=((1,), (0,)), precision=HIGH):
    return lax.dot_general(a, b, (dims, ((), ())), precision=precision, preferred_element_type=F32)


def iota(shape, dim):
    return lax.broadcasted_iota(jnp.int32, shape, dim)


def kernel(
    spec_hbm, core_hbm, fin_hbm, first_hbm, second_hbm, third_hbm,
    yr,
    spec, core, fin_ref, fin, first_ref, second_ref, third_ref, xs, xp, xr, bs, br, cs, cr, ys, stage, fr, sr, m1, m2, coef,
    in_sem, fac_send, fac_recv, b_send, b_recv, p_send, p_recv, x_send, x_recv, c_send, c_recv, y_send, y_recv, y_own,
):
    z, my, col = lax.axis_index("mx"), lax.axis_index("my"), lax.axis_index("col")
    h, e = my // 2, my % 2
    l, x = col // 4, col % 4
    kz = z * 4 + x

    loads = [
        pltpu.make_async_copy(far, here, in_sem.at[n])
        for n, (far, here) in enumerate((
            (fin_hbm, fin_ref), (spec_hbm, spec), (first_hbm, first_ref),
            (second_hbm, second_ref), (third_hbm, third_ref), (core_hbm, core),
        ))
    ]
    for load in loads:
        load.start()

    def plane(i):
        d = i + 1
        return (z + d // 8) % 4, my, ((l + (d // 4) % 2) % 2) * 4 + (x + d % 4) % 4

    def square(i):
        d = i + 1
        return z, ((h + d // 4) % 2) * 2 + (e + d % 2) % 2, ((l + (d // 2) % 2) % 2) * 4 + x

    barrier = pltpu.get_barrier_semaphore()

    def greet_plane(i, carry):
        pl.semaphore_signal(barrier, inc=1, device_id=plane(i), device_id_type=MESH)
        return carry

    def greet_square(i, carry):
        d = i + jnp.where(i >= 1, 1, 0)
        pl.semaphore_signal(barrier, inc=1, device_id=square(d), device_id_type=MESH)
        return carry

    lax.fori_loop(0, 31, greet_plane, 0)
    lax.fori_loop(0, 6, greet_square, 0)

    loads[0].wait()
    loads[1].wait()
    for a in range(16):
        true = (a // 8) * 32 + (a % 4) * 8 + (a // 4 % 2) * 4
        fin[4 * a : 4 * a + 4, :] = fin_ref[true : true + 4, :]
    xs2 = xs.reshape(2048, 128)

    def project(bk, carry):
        b, k = bk // 8, bk % 8
        real = dot(fin[...], spec[pl.ds(b * 1024 + k, 128, stride=8), :])
        imag = dot(fin[...], spec[pl.ds((2 + b) * 1024 + k, 128, stride=8), :])
        xs2[pl.ds(bk, 128, stride=16), :] = jnp.concatenate([real, imag], axis=0).T
        return carry

    lax.fori_loop(0, 16, project, 0)

    for load in loads[2:5]:
        load.wait()
    stage[...] = jnp.zeros_like(stage)
    stage[0, :, 0:16] = first_ref[...]
    stage[1, :, 0:16] = second_ref[...]
    fr[pl.ds(z, 1)] = stage[0:1]
    sr[pl.ds(my, 1)] = stage[1:2]

    pl.semaphore_wait(barrier, 37)

    swap = pltpu.make_async_remote_copy(
        xs.at[1 - l], xp, p_send, p_recv,
        device_id=(z, my, (1 - l) * 4 + x), device_id_type=MESH,
    )
    swap.start()

    def send_first(i, carry):
        pltpu.make_async_remote_copy(
            stage.at[0], fr.at[z], fac_send.at[0], fac_recv.at[0],
            device_id=((z + i + 1) % 4, my, col), device_id_type=MESH,
        ).start()
        d = i + 1
        pltpu.make_async_remote_copy(
            stage.at[1], sr.at[my], fac_send.at[1], fac_recv.at[1],
            device_id=(z, ((h + d // 2) % 2) * 2 + (e + d % 2) % 2, col), device_id_type=MESH,
        ).start()
        return carry

    lax.fori_loop(0, 3, send_first, 0)

    spread = jnp.where(iota((16, 256), 1) % 16 == iota((16, 256), 0), 1.0, 0.0)
    wide = dot(third_ref[...], spread, precision=HIGHEST)
    wide = jnp.broadcast_to(wide[:, None, :], (16, 16, 256)).reshape(256, 256)
    m1[...] = jnp.where(iota((256, 256), 0) % 16 == iota((256, 256), 1) // 16, wide, 0.0)
    loads[5].wait()

    def first_exchange(half, carry):
        def third_step(p, inner):
            both = jnp.concatenate([core[0, half * 4 + p], core[1, half * 4 + p]], axis=1)
            bs[:, half, p] = dot(m1[...], both).reshape(16, 16, 128)
            return inner

        lax.fori_loop(0, 4, third_step, 0)

        def send_b(i, inner):
            d = i + 1
            tz, tx = (z + d // 4) % 4, (x + d % 4) % 4
            pltpu.make_async_remote_copy(
                bs.at[tz * 4 + tx, half], br.at[half, z, x], b_send, b_recv.at[half],
                device_id=(tz, my, l * 4 + tx), device_id_type=MESH,
            ).start()
            return inner

        lax.fori_loop(0, 15, send_b, 0)
        br[half, z, x] = bs[kz, half]
        return carry

    lax.fori_loop(0, 2, first_exchange, 0)

    pltpu.make_async_copy(sr.at[0:3], sr.at[0:3], fac_recv.at[1]).wait()
    spread2 = jnp.where(iota((128, 128), 1) % 16 == iota((128, 128), 0), 1.0, 0.0)
    wide2 = dot(sr[...].reshape(32, 128), spread2, precision=HIGHEST)
    wide2 = jnp.broadcast_to(wide2[:, None, :], (32, 8, 128)).reshape(256, 128)
    m2[...] = jnp.where(iota((256, 128), 0) % 8 == iota((256, 128), 1) // 16, wide2, 0.0)

    def send_x(source, sample):
        def step(i, carry):
            d = i + 1
            tz, tx = (z + d // 4) % 4, (x + d % 4) % 4
            pltpu.make_async_remote_copy(
                source.at[:, tz * 4 + tx], xr.at[:, sample], x_send, x_recv,
                device_id=(tz, my, l * 4 + tx), device_id_type=MESH,
            ).start()
            return carry

        lax.fori_loop(0, 15, step, 0)
        for j in range(4):
            xr[j, sample] = source[j, kz]

    for half in range(2):
        pltpu.make_async_copy(bs.at[0:15, 0], bs.at[0:15, 0], b_recv.at[half]).wait()
        if half == 1:
            send_x(xs.at[l], z * 8 + col)

        def second_step(i, carry, half=half):
            zs, pair = i // 2, i % 2
            block = br[half, zs, pl.ds(pair * 2, 2)].reshape(128, 128)
            cs[half, :, :, zs, pl.ds(pair * 8, 8), :] = dot(m2[...], block).reshape(8, 4, 8, 128)
            return carry

        lax.fori_loop(0, 8, second_step, 0)

        def send_c(n, carry, half=half):
            j, i = n // 7, n % 7
            tz, tmy, tcol = square(i)
            pltpu.make_async_remote_copy(
                cs.at[half, tmy * 2 + tcol // 4, j],
                cr.at[j, :, my, pl.ds(l * 32 + half * 16, 16), :],
                c_send, c_recv.at[j],
                device_id=(tz, tmy, tcol), device_id_type=MESH,
            ).start()
            return carry

        lax.fori_loop(0, 28, send_c, 0)

        def keep_c(n, carry, half=half):
            j, zs = n // 4, n % 4
            cr[j, zs, my, pl.ds(l * 32 + half * 16, 16), :] = cs[half, my * 2 + l, j, zs]
            return carry

        lax.fori_loop(0, 16, keep_c, 0)

    swap.wait()
    send_x(xp, z * 8 + (1 - l) * 4 + x)

    pltpu.make_async_copy(sr.at[0:3], sr.at[0:3], fac_recv.at[0]).wait()
    for s in range(16):
        coef[s] = jnp.broadcast_to(fr[...].reshape(32, 128)[:, s : s + 1], (32, 128))
    pltpu.make_async_copy(xr.at[:, 0:30], xr.at[:, 0:30], x_recv).wait()

    sign = jnp.where(iota((64, 128), 1) < 64, -1.0, 1.0)

    def mode_step(j, carry):
        pltpu.make_async_copy(cs.at[:, 0:7, 0], cs.at[:, 0:7, 0], c_recv.at[j]).wait()
        rows = xr[j].reshape(512, 128)

        def group(g, inner):
            parts = []
            for i in range(4):
                top = cr[j, g, i]
                parts.append(jnp.concatenate([top, pltpu.roll(top, 64, 1) * sign], axis=0))
            prod = dot(rows, jnp.concatenate(parts, axis=1))
            total = None
            for i in range(4):
                piece = prod[:, i * 128 : (i + 1) * 128].reshape(4, 16, 8, 128)
                term = piece * coef[g * 4 + i].reshape(4, 1, 8, 128)
                total = term if total is None else total + term
            total = total.reshape(32, 16, 128)

            @pl.when(g == 0)
            def _():
                ys[j] = total

            @pl.when(g > 0)
            def _():
                ys[j] += total

            return inner

        lax.fori_loop(0, 4, group, 0)

        def send_y(i, inner):
            d = jnp.where(i < 16, (i // 4) * 8 + 4 + i % 4, ((i - 15) // 4) * 8 + (i - 15) % 4)
            tz, tmy, tcol = plane(d - 1)
            pltpu.make_async_remote_copy(
                ys.at[j, tz * 8 + tcol], yr.at[l, j, kz], y_send, y_recv,
                device_id=(tz, tmy, tcol), device_id_type=MESH,
            ).start()
            return inner

        lax.fori_loop(0, 31, send_y, 0)
        pltpu.make_async_copy(ys.at[j, z * 8 + col], yr.at[l, j, kz], y_own).start()
        return carry

    lax.fori_loop(0, 4, mode_step, 0)
    pltpu.make_async_copy(ys.at[:, 0], ys.at[:, 0], y_own).wait()
    pltpu.make_async_copy(ys.at[:, 0:31], ys.at[:, 0:31], y_recv).wait()
    pltpu.make_async_copy(sr.at[0:3], sr.at[0:3], fac_send.at[0]).wait()
    pltpu.make_async_copy(sr.at[0:3], sr.at[0:3], fac_send.at[1]).wait()
    pltpu.make_async_copy(bs.at[0:15], bs.at[0:15], b_send).wait()
    pltpu.make_async_copy(xr.at[:, 0:30], xr.at[:, 0:30], x_send).wait()
    pltpu.make_async_copy(cs.at[:, 0:7], cs.at[:, 0:7], c_send).wait()
    pltpu.make_async_copy(ys.at[:, 0:31], ys.at[:, 0:31], y_send).wait()


def finish_kernel(modes_ref, fout_ref, out_ref):
    factor = fout_ref[...].T
    blank = jnp.zeros_like(factor)
    part = pl.program_id(0)
    left = jnp.where(part == 0, factor, blank)
    right = jnp.where(part == 0, blank, factor)
    wide = jnp.concatenate([left, right], axis=1)
    base = pl.program_id(1) * 8
    for k in range(8):
        modes = modes_ref[pl.ds(base + k, 128, stride=16), :]
        out_ref[pl.ds(k, 128, stride=8), :] = dot(wide, modes, ((1,), (1,)))


def per_device(
    spectrum, core_tensor, input_factor, output_factor, first_factor, second_factor, third_factor
):
    spec = spectrum.reshape(4096, 128)
    core = jnp.transpose(core_tensor[:, :, :, 0], (0, 1, 3, 4, 2)).reshape(2, 8, 256, 64)
    anywhere = pl.BlockSpec(memory_space=pl.ANY)
    vmem = lambda *shape: pltpu.VMEM(shape, F32)
    dma = pltpu.SemaphoreType.DMA
    values = pl.pallas_call(
        kernel,
        out_shape=jax.ShapeDtypeStruct((2, 4, 16, 16, 128), F32),
        in_specs=[anywhere] * 6,
        out_specs=anywhere,
        scratch_shapes=[
            vmem(4096, 128),
            vmem(2, 8, 256, 64),
            vmem(64, 128), vmem(64, 128), vmem(8, 16), vmem(8, 16), vmem(16, 16),
            vmem(2, 4, 16, 16, 128),
            vmem(4, 16, 16, 128),
            vmem(4, 32, 16, 128),
            vmem(16, 2, 4, 16, 128),
            vmem(2, 4, 4, 4, 16, 128),
            vmem(2, 8, 4, 4, 16, 128),
            vmem(4, 4, 4, 64, 128),
            vmem(4, 32, 16, 128),
            vmem(2, 8, 128),
            vmem(4, 8, 128),
            vmem(4, 8, 128),
            vmem(256, 256),
            vmem(256, 128),
            vmem(16, 32, 128),
            dma((6,)), dma((2,)), dma((2,)), dma, dma((2,)), dma, dma, dma, dma, dma, dma((4,)), dma, dma,
            dma,
        ],
        compiler_params=pltpu.CompilerParams(
            collective_id=0, has_side_effects=True, vmem_limit_bytes=63 * 1024 * 1024
        ),
    )(spec, core, input_factor.T, first_factor, second_factor, third_factor)
    out = pl.pallas_call(
        finish_kernel,
        grid=(2, 2),
        out_shape=jax.ShapeDtypeStruct((4096, 128), F32),
        in_specs=[
            pl.BlockSpec((2048, 128), lambda c, b: (0, 0)),
            pl.BlockSpec((64, 128), lambda c, b: (0, 0)),
        ],
        out_specs=pl.BlockSpec((1024, 128), lambda c, b: (c * 2 + b, 0)),
        compiler_params=pltpu.CompilerParams(vmem_limit_bytes=63 * 1024 * 1024),
    )(values.reshape(2048, 128), output_factor.T)
    return out.reshape(2, 2, 128, 8, 128)


def solution(mesh):
    placed = (
        P(None, "col", None, "mx", "my"),
        P(None, "col", None, ("mx", "my"), None, None),
        P(),
        P(),
        P("mx", None),
        P("my", None),
        P(),
    )
    return jax.shard_map(
        per_device,
        mesh=mesh,
        in_specs=placed,
        out_specs=P(None, "col", None, "mx", "my"),
        check_vma=False,
    )
```

time: 83.6 us -> 71.2 us (0.85)
  Pallas kernels: 80.3 us -> 71 us
  local copies, waits for them, and re-layouts: 3.05 us -> 0 us
    pallas_call x1 -> x2, Pallas kernels: 80.3 us -> 71 us  [the longest x1 65.9 us: per_device(): pl.pallas_call(kernel, out_shape=jax.ShapeDtypeStruct((2, 4, 16, 16, 128)...]
    unnamed x1 -> x0, local copies, waits for them, and re-layouts: 3.05 us -> none
where the time goes in v1:
time: 71.2 us; the launch traced here: 71.1 us
  Pallas kernels  71 us (100%)
    pallas_call x1, Pallas kernels, per_device(): pl.pallas_call(kernel, out_shape=jax.ShapeDtypeStruct((2, 4, 16, 16, 128)...  65.9 us
    pallas_call x1, Pallas kernels, per_device(): pl.pallas_call(finish_kernel, grid=(2, 2), out_shape=jax.ShapeDtypeStruct...  5.17 us

profile of v1, /device:TPU:1, one launch (start us, length us, event | category | flops | bytes accessed | tf_op | source)
XLA Modules:
  0.0 71.1 jit_solution(346950693259710632)
XLA Ops:
  0.0 65.9 %shard_map.73 = f32[2,4,16,16,128]{4,3,2,1,0:T(8,128)} custom-call(f32[4096,128]{1,0:T(8,128)} %bitcast.11, f32[2,8,256,64]{3,2,1,0:T(8,128)} %bitcast.12, f32[64,128]{1,0:T(8,128)} %bitcast.13, f32[8,16]{1,0:T(8,128)} %first_hbm.1, f32[8,16]{1,0:T(8,128)} %second_hbm.1, f32[16,16]{1,0:T(8,128)} %third_hbm.1), custom_call_target="tpu_custom_call" | custom-call | tf_op jit(solution)/shard_map/pallas_call | solution.py:277
  65.9 5.2 %shard_map.74 = f32[4096,128]{1,0:T(8,128)} custom-call(f32[2048,128]{1,0:T(8,128)} %bitcast.10, f32[64,128]{1,0:T(8,128)} %bitcast.14), custom_call_target="tpu_custom_call" | custom-call | tf_op jit(solution)/shard_map/pallas_call | solution.py:307

commit v2 on v1

--- a/solution.py
+++ b/solution.py
@@ -6,13 +6,24 @@
 from jax.sharding import PartitionSpec as P
 
 MESH = pl.DeviceIdType.MESH
-HIGH = lax.Precision.HIGH
-HIGHEST = lax.Precision.HIGHEST
 F32 = jnp.float32
 
 
-def dot(a, b, dims=((1,), (0,)), precision=HIGH):
-    return lax.dot_general(a, b, (dims, ((), ())), precision=precision, preferred_element_type=F32)
+def exact(a, b):
+    return lax.dot_general(
+        a, b, (((1,), (0,)), ((), ())), precision=lax.Precision.HIGHEST, preferred_element_type=F32
+    )
+
+
+def split(a):
+    high = a.astype(jnp.bfloat16)
+    return high, (a - high.astype(F32)).astype(jnp.bfloat16)
+
+
+def dot(a, b, dims=((1,), (0,))):
+    (ah, al), (bh, bl) = split(a), split(b)
+    one = lambda u, v: lax.dot_general(u, v, (dims, ((), ())), preferred_element_type=F32)
+    return one(ah, bh) + (one(al, bh) + one(ah, bl))
 
 
 def iota(shape, dim):
@@ -33,8 +44,11 @@
     loads = [
         pltpu.make_async_copy(far, here, in_sem.at[n])
         for n, (far, here) in enumerate((
-            (fin_hbm, fin_ref), (spec_hbm, spec), (first_hbm, first_ref),
-            (second_hbm, second_ref), (third_hbm, third_ref), (core_hbm, core),
+            (fin_hbm, fin_ref),
+            (spec_hbm.at[:, 0], spec.at[:, 0]),
+            (spec_hbm.at[:, 1], spec.at[:, 1]),
+            (first_hbm, first_ref), (second_hbm, second_ref), (third_hbm, third_ref),
+            (core_hbm, core),
         ))
     ]
     for load in loads:
@@ -63,36 +77,45 @@
     lax.fori_loop(0, 6, greet_square, 0)
 
     loads[0].wait()
-    loads[1].wait()
     for a in range(16):
         true = (a // 8) * 32 + (a % 4) * 8 + (a // 4 % 2) * 4
         fin[4 * a : 4 * a + 4, :] = fin_ref[true : true + 4, :]
     xs2 = xs.reshape(2048, 128)
 
-    def project(bk, carry):
-        b, k = bk // 8, bk % 8
-        real = dot(fin[...], spec[pl.ds(b * 1024 + k, 128, stride=8), :])
-        imag = dot(fin[...], spec[pl.ds((2 + b) * 1024 + k, 128, stride=8), :])
-        xs2[pl.ds(bk, 128, stride=16), :] = jnp.concatenate([real, imag], axis=0).T
-        return carry
-
-    lax.fori_loop(0, 16, project, 0)
-
-    for load in loads[2:5]:
+    def project(b):
+        loads[1 + b].wait()
+
+        def step(n, carry):
+            for k in range(4):
+                k = n * 4 + k
+                real = dot(fin[...], spec[0, b, pl.ds(k, 128, stride=8), :])
+                imag = dot(fin[...], spec[1, b, pl.ds(k, 128, stride=8), :])
+                both = jnp.concatenate([real, imag], axis=0).T
+                xs2[pl.ds(b * 8 + k, 128, stride=16), :] = both
+            return carry
+
+        lax.fori_loop(0, 2, step, 0)
+
+    def swap(b):
+        half = pl.ds(b * 8, 8)
+        return pltpu.make_async_remote_copy(
+            xs.at[1 - l, :, :, half], xp.at[:, :, half], p_send.at[b], p_recv.at[b],
+            device_id=(z, my, (1 - l) * 4 + x), device_id_type=MESH,
+        )
+
+    project(0)
+    pl.semaphore_wait(barrier, 37)
+    swap(0).start()
+    project(1)
+    swap(1).start()
+
+    for load in loads[3:6]:
         load.wait()
     stage[...] = jnp.zeros_like(stage)
     stage[0, :, 0:16] = first_ref[...]
     stage[1, :, 0:16] = second_ref[...]
     fr[pl.ds(z, 1)] = stage[0:1]
     sr[pl.ds(my, 1)] = stage[1:2]
-
-    pl.semaphore_wait(barrier, 37)
-
-    swap = pltpu.make_async_remote_copy(
-        xs.at[1 - l], xp, p_send, p_recv,
-        device_id=(z, my, (1 - l) * 4 + x), device_id_type=MESH,
-    )
-    swap.start()
 
     def send_first(i, carry):
         pltpu.make_async_remote_copy(
@@ -109,18 +132,15 @@
     lax.fori_loop(0, 3, send_first, 0)
 
     spread = jnp.where(iota((16, 256), 1) % 16 == iota((16, 256), 0), 1.0, 0.0)
-    wide = dot(third_ref[...], spread, precision=HIGHEST)
+    wide = exact(third_ref[...], spread)
     wide = jnp.broadcast_to(wide[:, None, :], (16, 16, 256)).reshape(256, 256)
     m1[...] = jnp.where(iota((256, 256), 0) % 16 == iota((256, 256), 1) // 16, wide, 0.0)
-    loads[5].wait()
+    loads[6].wait()
 
     def first_exchange(half, carry):
-        def third_step(p, inner):
+        for p in range(4):
             both = jnp.concatenate([core[0, half * 4 + p], core[1, half * 4 + p]], axis=1)
             bs[:, half, p] = dot(m1[...], both).reshape(16, 16, 128)
-            return inner
-
-        lax.fori_loop(0, 4, third_step, 0)
 
         def send_b(i, inner):
             d = i + 1
@@ -139,7 +159,7 @@
 
     pltpu.make_async_copy(sr.at[0:3], sr.at[0:3], fac_recv.at[1]).wait()
     spread2 = jnp.where(iota((128, 128), 1) % 16 == iota((128, 128), 0), 1.0, 0.0)
-    wide2 = dot(sr[...].reshape(32, 128), spread2, precision=HIGHEST)
+    wide2 = exact(sr[...].reshape(32, 128), spread2)
     wide2 = jnp.broadcast_to(wide2[:, None, :], (32, 8, 128)).reshape(256, 128)
     m2[...] = jnp.where(iota((256, 128), 0) % 8 == iota((256, 128), 1) // 16, wide2, 0.0)
 
@@ -162,13 +182,15 @@
         if half == 1:
             send_x(xs.at[l], z * 8 + col)
 
-        def second_step(i, carry, half=half):
-            zs, pair = i // 2, i % 2
-            block = br[half, zs, pl.ds(pair * 2, 2)].reshape(128, 128)
-            cs[half, :, :, zs, pl.ds(pair * 8, 8), :] = dot(m2[...], block).reshape(8, 4, 8, 128)
-            return carry
-
-        lax.fori_loop(0, 8, second_step, 0)
+        def second_step(n, carry, half=half):
+            for i in range(4):
+                zs, pair = n * 2 + i // 2, i % 2
+                block = br[half, zs, pl.ds(pair * 2, 2)].reshape(128, 128)
+                part = dot(m2[...], block).reshape(8, 4, 8, 128)
+                cs[half, :, :, zs, pl.ds(pair * 8, 8), :] = part
+            return carry
+
+        lax.fori_loop(0, 2, second_step, 0)
 
         def send_c(n, carry, half=half):
             j, i = n // 7, n % 7
@@ -190,7 +212,8 @@
 
         lax.fori_loop(0, 16, keep_c, 0)
 
-    swap.wait()
+    swap(0).wait()
+    swap(1).wait()
     send_x(xp, z * 8 + (1 - l) * 4 + x)
 
     pltpu.make_async_copy(sr.at[0:3], sr.at[0:3], fac_recv.at[0]).wait()
@@ -256,20 +279,20 @@
 def finish_kernel(modes_ref, fout_ref, out_ref):
     factor = fout_ref[...].T
     blank = jnp.zeros_like(factor)
-    part = pl.program_id(0)
-    left = jnp.where(part == 0, factor, blank)
-    right = jnp.where(part == 0, blank, factor)
-    wide = jnp.concatenate([left, right], axis=1)
-    base = pl.program_id(1) * 8
+    wide = jnp.concatenate(
+        [jnp.concatenate([factor, blank], axis=1), jnp.concatenate([blank, factor], axis=1)], axis=0
+    )
+    modes = modes_ref.reshape(1024, 128)
     for k in range(8):
-        modes = modes_ref[pl.ds(base + k, 128, stride=16), :]
-        out_ref[pl.ds(k, 128, stride=8), :] = dot(wide, modes, ((1,), (1,)))
+        mixed = dot(wide, modes[pl.ds(k, 128, stride=8), :], ((1,), (1,)))
+        out_ref[0, 0, pl.ds(k, 128, stride=8), :] = mixed[0:128]
+        out_ref[1, 0, pl.ds(k, 128, stride=8), :] = mixed[128:256]
 
 
 def per_device(
     spectrum, core_tensor, input_factor, output_factor, first_factor, second_factor, third_factor
 ):
-    spec = spectrum.reshape(4096, 128)
+    spec = spectrum.reshape(2, 2, 1024, 128)
     core = jnp.transpose(core_tensor[:, :, :, 0], (0, 1, 3, 4, 2)).reshape(2, 8, 256, 64)
     anywhere = pl.BlockSpec(memory_space=pl.ANY)
     vmem = lambda *shape: pltpu.VMEM(shape, F32)
@@ -280,7 +303,7 @@
         in_specs=[anywhere] * 6,
         out_specs=anywhere,
         scratch_shapes=[
-            vmem(4096, 128),
+            vmem(2, 2, 1024, 128),
             vmem(2, 8, 256, 64),
             vmem(64, 128), vmem(64, 128), vmem(8, 16), vmem(8, 16), vmem(16, 16),
             vmem(2, 4, 16, 16, 128),
@@ -297,7 +320,7 @@
             vmem(256, 256),
             vmem(256, 128),
             vmem(16, 32, 128),
-            dma((6,)), dma((2,)), dma((2,)), dma, dma((2,)), dma, dma, dma, dma, dma, dma((4,)), dma, dma,
+            dma((7,)), dma((2,)), dma((2,)), dma, dma((2,)), dma((2,)), dma((2,)), dma, dma, dma, dma((4,)), dma, dma,
             dma,
         ],
         compiler_params=pltpu.CompilerParams(
@@ -306,15 +329,15 @@
     )(spec, core, input_factor.T, first_factor, second_factor, third_factor)
     out = pl.pallas_call(
         finish_kernel,
-        grid=(2, 2),
-        out_shape=jax.ShapeDtypeStruct((4096, 128), F32),
+        grid=(2,),
+        out_shape=jax.ShapeDtypeStruct((2, 2, 1024, 128), F32),
         in_specs=[
-            pl.BlockSpec((2048, 128), lambda c, b: (0, 0)),
-            pl.BlockSpec((64, 128), lambda c, b: (0, 0)),
+            pl.BlockSpec((128, 1, 8, 128), lambda b: (0, b, 0, 0)),
+            pl.BlockSpec((64, 128), lambda b: (0, 0)),
         ],
-        out_specs=pl.BlockSpec((1024, 128), lambda c, b: (c * 2 + b, 0)),
+        out_specs=pl.BlockSpec((2, 1, 1024, 128), lambda b: (0, b, 0, 0)),
         compiler_params=pltpu.CompilerParams(vmem_limit_bytes=63 * 1024 * 1024),
-    )(values.reshape(2048, 128), output_factor.T)
+    )(values.reshape(128, 2, 8, 128), output_factor.T)
     return out.reshape(2, 2, 128, 8, 128)
 
 

time: 71.2 us -> 66.3 us (0.931)
  Pallas kernels: 71 us -> 66.1 us
    pallas_call x1, Pallas kernels: 65.9 us -> 62.7 us  [per_device(): pl.pallas_call(kernel, out_shape=jax.ShapeDtypeStruct((2, 4, 16, 16, 128)...]
    pallas_call x1, Pallas kernels: 5.17 us -> 3.46 us  [per_device(): pl.pallas_call(finish_kernel, grid=(2,), out_shape=jax.ShapeDtypeStruct((...]
where the time goes in v2:
time: 66.3 us; the launch traced here: 66.1 us
  Pallas kernels  66.1 us (100%)
    pallas_call x1, Pallas kernels, per_device(): pl.pallas_call(kernel, out_shape=jax.ShapeDtypeStruct((2, 4, 16, 16, 128)...  62.7 us
    pallas_call x1, Pallas kernels, per_device(): pl.pallas_call(finish_kernel, grid=(2,), out_shape=jax.ShapeDtypeStruct((...  3.46 us

profile of v2, /device:TPU:1, one launch (start us, length us, event | category | flops | bytes accessed | tf_op | source)
XLA Modules:
  0.0 66.1 jit_solution(581221051468970582)
XLA Ops:
  0.0 62.7 %shard_map.73 = f32[2,4,16,16,128]{4,3,2,1,0:T(8,128)} custom-call(f32[2,2,1024,128]{3,2,1,0:T(8,128)} %bitcast.11, f32[2,8,256,64]{3,2,1,0:T(8,128)} %bitcast.12, f32[64,128]{1,0:T(8,128)} %bitcast.13, f32[8,16]{1,0:T(8,128)} %first_hbm.1, f32[8,16]{1,0:T(8,128)} %second_hbm.1, f32[16,16]{1,0:T(8,128)} %third_hbm.1), custom_call_target="tpu_custom_call" | custom-call | tf_op jit(solution)/shard_map/pallas_call | solution.py:300
  62.7 3.5 %shard_map.74 = f32[2,2,1024,128]{3,2,1,0:T(8,128)} custom-call(f32[128,2,8,128]{3,2,1,0:T(8,128)} %bitcast.10, f32[64,128]{1,0:T(8,128)} %bitcast.14), custom_call_target="tpu_custom_call" | custom-call | tf_op jit(solution)/shard_map/pallas_call | solution.py:330

commit v3 on v2

--- a/solution.py
+++ b/solution.py
@@ -48,39 +48,41 @@
             (spec_hbm.at[:, 0], spec.at[:, 0]),
             (spec_hbm.at[:, 1], spec.at[:, 1]),
             (first_hbm, first_ref), (second_hbm, second_ref), (third_hbm, third_ref),
-            (core_hbm, core),
+            (core_hbm.at[:, 0:4], core.at[:, 0:4]),
+            (core_hbm.at[:, 4:8], core.at[:, 4:8]),
         ))
     ]
-    for load in loads:
-        load.start()
+    for n in (5, 6, 0, 1, 3, 4, 7, 2):
+        loads[n].start()
+
+    rem, div = lax.rem, lax.div
 
     def plane(i):
-        d = i + 1
-        return (z + d // 8) % 4, my, ((l + (d // 4) % 2) % 2) * 4 + (x + d % 4) % 4
+        d = jnp.int32(i + 1)
+        return rem(z + div(d, 8), 4), my, rem(l + rem(div(d, 4), 2), 2) * 4 + rem(x + rem(d, 4), 4)
 
     def square(i):
-        d = i + 1
-        return z, ((h + d // 4) % 2) * 2 + (e + d % 2) % 2, ((l + (d // 2) % 2) % 2) * 4 + x
+        d = jnp.int32(i + 1)
+        return (
+            z,
+            rem(h + div(d, 4), 2) * 2 + rem(e + rem(d, 2), 2),
+            rem(l + rem(div(d, 2), 2), 2) * 4 + x,
+        )
 
     barrier = pltpu.get_barrier_semaphore()
 
-    def greet_plane(i, carry):
-        pl.semaphore_signal(barrier, inc=1, device_id=plane(i), device_id_type=MESH)
-        return carry
-
-    def greet_square(i, carry):
-        d = i + jnp.where(i >= 1, 1, 0)
-        pl.semaphore_signal(barrier, inc=1, device_id=square(d), device_id_type=MESH)
-        return carry
-
-    lax.fori_loop(0, 31, greet_plane, 0)
-    lax.fori_loop(0, 6, greet_square, 0)
+    def hops(d):
+        return (0, 1, 2, 1)[d // 8] + (d // 4) % 2 + (0, 1, 2, 1)[d % 4]
+
+    for d in sorted(range(1, 32), key=lambda d: -hops(d)):
+        pl.semaphore_signal(barrier, inc=1, device_id=plane(d - 1), device_id_type=MESH)
+    for d in (4, 5, 6, 7, 3, 1):
+        pl.semaphore_signal(barrier, inc=1, device_id=square(d - 1), device_id_type=MESH)
 
     loads[0].wait()
     for a in range(16):
         true = (a // 8) * 32 + (a % 4) * 8 + (a // 4 % 2) * 4
         fin[4 * a : 4 * a + 4, :] = fin_ref[true : true + 4, :]
-    xs2 = xs.reshape(2048, 128)
 
     def project(b):
         loads[1 + b].wait()
@@ -91,31 +93,61 @@
                 real = dot(fin[...], spec[0, b, pl.ds(k, 128, stride=8), :])
                 imag = dot(fin[...], spec[1, b, pl.ds(k, 128, stride=8), :])
                 both = jnp.concatenate([real, imag], axis=0).T
-                xs2[pl.ds(b * 8 + k, 128, stride=16), :] = both
+                for part in range(2):
+                    rows = xs.at[part, b].reshape(512, 128)
+                    rows[pl.ds(k, 64, stride=8), :] = both[part * 64 : part * 64 + 64]
             return carry
 
         lax.fori_loop(0, 2, step, 0)
 
     def swap(b):
-        half = pl.ds(b * 8, 8)
         return pltpu.make_async_remote_copy(
-            xs.at[1 - l, :, :, half], xp.at[:, :, half], p_send.at[b], p_recv.at[b],
+            xs.at[1 - l, b], xp.at[b], p_send.at[b], p_recv.at[b],
             device_id=(z, my, (1 - l) * 4 + x), device_id_type=MESH,
         )
 
-    project(0)
-    pl.semaphore_wait(barrier, 37)
-    swap(0).start()
-    project(1)
-    swap(1).start()
-
-    for load in loads[3:6]:
+    for load in loads[3:5]:
         load.wait()
     stage[...] = jnp.zeros_like(stage)
     stage[0, :, 0:16] = first_ref[...]
     stage[1, :, 0:16] = second_ref[...]
     fr[pl.ds(z, 1)] = stage[0:1]
     sr[pl.ds(my, 1)] = stage[1:2]
+
+    loads[5].wait()
+    spread = jnp.where(iota((16, 256), 1) % 16 == iota((16, 256), 0), 1.0, 0.0)
+    wide = exact(third_ref[...], spread)
+    wide = jnp.broadcast_to(wide[:, None, :], (16, 16, 256)).reshape(256, 256)
+    m1[...] = jnp.where(iota((256, 256), 0) % 16 == iota((256, 256), 1) // 16, wide, 0.0)
+
+    def third_step(half):
+        loads[6 + half].wait()
+        for p in range(4):
+            both = jnp.concatenate([core[0, half * 4 + p], core[1, half * 4 + p]], axis=1)
+            bs[:, half, p] = dot(m1[...], both).reshape(16, 16, 128)
+
+    def send_b(half):
+        def step(i, carry):
+            d = i + 1
+            tz, tx = lax.rem(z + lax.div(d, 4), 4), lax.rem(x + lax.rem(d, 4), 4)
+            pltpu.make_async_remote_copy(
+                bs.at[tz * 4 + tx, half], br.at[half, z, x], b_send, b_recv.at[half],
+                device_id=(tz, my, l * 4 + tx), device_id_type=MESH,
+            ).start()
+            return carry
+
+        lax.fori_loop(0, 15, step, 0)
+        br[half, z, x] = bs[kz, half]
+
+    third_step(0)
+    project(0)
+    pl.semaphore_wait(barrier, 37)
+    swap(0).start()
+    send_b(0)
+    third_step(1)
+    send_b(1)
+    project(1)
+    swap(1).start()
 
     def send_first(i, carry):
         pltpu.make_async_remote_copy(
@@ -131,32 +163,6 @@
 
     lax.fori_loop(0, 3, send_first, 0)
 
-    spread = jnp.where(iota((16, 256), 1) % 16 == iota((16, 256), 0), 1.0, 0.0)
-    wide = exact(third_ref[...], spread)
-    wide = jnp.broadcast_to(wide[:, None, :], (16, 16, 256)).reshape(256, 256)
-    m1[...] = jnp.where(iota((256, 256), 0) % 16 == iota((256, 256), 1) // 16, wide, 0.0)
-    loads[6].wait()
-
-    def first_exchange(half, carry):
-        for p in range(4):
-            both = jnp.concatenate([core[0, half * 4 + p], core[1, half * 4 + p]], axis=1)
-            bs[:, half, p] = dot(m1[...], both).reshape(16, 16, 128)
-
-        def send_b(i, inner):
-            d = i + 1
-            tz, tx = (z + d // 4) % 4, (x + d % 4) % 4
-            pltpu.make_async_remote_copy(
-                bs.at[tz * 4 + tx, half], br.at[half, z, x], b_send, b_recv.at[half],
-                device_id=(tz, my, l * 4 + tx), device_id_type=MESH,
-            ).start()
-            return inner
-
-        lax.fori_loop(0, 15, send_b, 0)
-        br[half, z, x] = bs[kz, half]
-        return carry
-
-    lax.fori_loop(0, 2, first_exchange, 0)
-
     pltpu.make_async_copy(sr.at[0:3], sr.at[0:3], fac_recv.at[1]).wait()
     spread2 = jnp.where(iota((128, 128), 1) % 16 == iota((128, 128), 0), 1.0, 0.0)
     wide2 = exact(sr[...].reshape(32, 128), spread2)
@@ -168,14 +174,15 @@
             d = i + 1
             tz, tx = (z + d // 4) % 4, (x + d % 4) % 4
             pltpu.make_async_remote_copy(
-                source.at[:, tz * 4 + tx], xr.at[:, sample], x_send, x_recv,
+                source.at[:, :, tz * 4 + tx], xr.at[:, :, sample], x_send, x_recv,
                 device_id=(tz, my, l * 4 + tx), device_id_type=MESH,
             ).start()
             return carry
 
         lax.fori_loop(0, 15, step, 0)
-        for j in range(4):
-            xr[j, sample] = source[j, kz]
+        for b in range(2):
+            for j in range(4):
+                xr[b, j, sample] = source[b, j, kz]
 
     for half in range(2):
         pltpu.make_async_copy(bs.at[0:15, 0], bs.at[0:15, 0], b_recv.at[half]).wait()
@@ -197,7 +204,7 @@
             tz, tmy, tcol = square(i)
             pltpu.make_async_remote_copy(
                 cs.at[half, tmy * 2 + tcol // 4, j],
-                cr.at[j, :, my, pl.ds(l * 32 + half * 16, 16), :],
+                cr.at[j, my, l, half],
                 c_send, c_recv.at[j],
                 device_id=(tz, tmy, tcol), device_id_type=MESH,
             ).start()
@@ -207,7 +214,7 @@
 
         def keep_c(n, carry, half=half):
             j, zs = n // 4, n % 4
-            cr[j, zs, my, pl.ds(l * 32 + half * 16, 16), :] = cs[half, my * 2 + l, j, zs]
+            cr[j, my, l, half, zs] = cs[half, my * 2 + l, j, zs]
             return carry
 
         lax.fori_loop(0, 16, keep_c, 0)
@@ -219,38 +226,40 @@
     pltpu.make_async_copy(sr.at[0:3], sr.at[0:3], fac_recv.at[0]).wait()
     for s in range(16):
         coef[s] = jnp.broadcast_to(fr[...].reshape(32, 128)[:, s : s + 1], (32, 128))
-    pltpu.make_async_copy(xr.at[:, 0:30], xr.at[:, 0:30], x_recv).wait()
+    pltpu.make_async_copy(xr.at[:, :, 0:30], xr.at[:, :, 0:30], x_recv).wait()
 
     sign = jnp.where(iota((64, 128), 1) < 64, -1.0, 1.0)
 
     def mode_step(j, carry):
         pltpu.make_async_copy(cs.at[:, 0:7, 0], cs.at[:, 0:7, 0], c_recv.at[j]).wait()
-        rows = xr[j].reshape(512, 128)
-
-        def group(g, inner):
+        high, low = split(xr[:, j].reshape(512, 128))
+        both = jnp.concatenate([high, low], axis=1)
+
+        def group(g):
             parts = []
             for i in range(4):
-                top = cr[j, g, i]
+                top = cr[j, i, :, :, g].reshape(64, 128)
                 parts.append(jnp.concatenate([top, pltpu.roll(top, 64, 1) * sign], axis=0))
-            prod = dot(rows, jnp.concatenate(parts, axis=1))
+            upper, lower = split(jnp.concatenate(parts, axis=1))
+            twice = jnp.concatenate([upper, upper], axis=0)
+            one = lambda u, v: lax.dot_general(
+                u, v, (((1,), (0,)), ((), ())), preferred_element_type=F32
+            )
+            prod = one(both, twice) + one(high, lower)
             total = None
             for i in range(4):
-                piece = prod[:, i * 128 : (i + 1) * 128].reshape(4, 16, 8, 128)
-                term = piece * coef[g * 4 + i].reshape(4, 1, 8, 128)
+                piece = prod[:, i * 128 : (i + 1) * 128].reshape(2, 4, 8, 8, 128)
+                term = piece * coef[g * 4 + i].reshape(1, 4, 1, 8, 128)
                 total = term if total is None else total + term
-            total = total.reshape(32, 16, 128)
-
-            @pl.when(g == 0)
-            def _():
-                ys[j] = total
-
-            @pl.when(g > 0)
-            def _():
-                ys[j] += total
-
-            return inner
-
-        lax.fori_loop(0, 4, group, 0)
+            return total.reshape(2, 32, 8, 128)
+
+        for g in range(4):
+            total = group(g)
+            for b in range(2):
+                if g == 0:
+                    ys[j, :, b] = total[b]
+                else:
+                    ys[j, :, b] += total[b]
 
         def send_y(i, inner):
             d = jnp.where(i < 16, (i // 4) * 8 + 4 + i % 4, ((i - 15) // 4) * 8 + (i - 15) % 4)
@@ -271,7 +280,7 @@
     pltpu.make_async_copy(sr.at[0:3], sr.at[0:3], fac_send.at[0]).wait()
     pltpu.make_async_copy(sr.at[0:3], sr.at[0:3], fac_send.at[1]).wait()
     pltpu.make_async_copy(bs.at[0:15], bs.at[0:15], b_send).wait()
-    pltpu.make_async_copy(xr.at[:, 0:30], xr.at[:, 0:30], x_send).wait()
+    pltpu.make_async_copy(xr.at[:, :, 0:30], xr.at[:, :, 0:30], x_send).wait()
     pltpu.make_async_copy(cs.at[:, 0:7], cs.at[:, 0:7], c_send).wait()
     pltpu.make_async_copy(ys.at[:, 0:31], ys.at[:, 0:31], y_send).wait()
 
@@ -299,28 +308,28 @@
     dma = pltpu.SemaphoreType.DMA
     values = pl.pallas_call(
         kernel,
-        out_shape=jax.ShapeDtypeStruct((2, 4, 16, 16, 128), F32),
+        out_shape=jax.ShapeDtypeStruct((2, 4, 16, 2, 8, 128), F32),
         in_specs=[anywhere] * 6,
         out_specs=anywhere,
         scratch_shapes=[
             vmem(2, 2, 1024, 128),
             vmem(2, 8, 256, 64),
             vmem(64, 128), vmem(64, 128), vmem(8, 16), vmem(8, 16), vmem(16, 16),
-            vmem(2, 4, 16, 16, 128),
-            vmem(4, 16, 16, 128),
-            vmem(4, 32, 16, 128),
+            vmem(2, 2, 4, 16, 8, 128),
+            vmem(2, 4, 16, 8, 128),
+            vmem(2, 4, 32, 8, 128),
             vmem(16, 2, 4, 16, 128),
             vmem(2, 4, 4, 4, 16, 128),
             vmem(2, 8, 4, 4, 16, 128),
-            vmem(4, 4, 4, 64, 128),
-            vmem(4, 32, 16, 128),
+            vmem(4, 4, 2, 2, 4, 16, 128),
+            vmem(4, 32, 2, 8, 128),
             vmem(2, 8, 128),
             vmem(4, 8, 128),
             vmem(4, 8, 128),
             vmem(256, 256),
             vmem(256, 128),
             vmem(16, 32, 128),
-            dma((7,)), dma((2,)), dma((2,)), dma, dma((2,)), dma((2,)), dma((2,)), dma, dma, dma, dma((4,)), dma, dma,
+            dma((8,)), dma((2,)), dma((2,)), dma, dma((2,)), dma((2,)), dma((2,)), dma, dma, dma, dma((4,)), dma, dma,
             dma,
         ],
         compiler_params=pltpu.CompilerParams(

time: 66.3 us -> 65.2 us (0.983)
  Pallas kernels: 66.1 us -> 64.5 us
    pallas_call x1, Pallas kernels: 62.7 us -> 61 us  [per_device(): pl.pallas_call(kernel, out_shape=jax.ShapeDtypeStruct((2, 4, 16, 2, 8, 12...]
where the time goes in v3:
time: 65.2 us; the launch traced here: 64.5 us
  Pallas kernels  64.5 us (99%)
    pallas_call x1, Pallas kernels, per_device(): pl.pallas_call(kernel, out_shape=jax.ShapeDtypeStruct((2, 4, 16, 2, 8, 12...  61 us
    pallas_call x1, Pallas kernels, per_device(): pl.pallas_call(finish_kernel, grid=(2,), out_shape=jax.ShapeDtypeStruct((...  3.45 us

profile of v3, /device:TPU:1, one launch (start us, length us, event | category | flops | bytes accessed | tf_op | source)
XLA Modules:
  0.0 64.5 jit_solution(16360826965661535451)
XLA Ops:
  0.0 61.0 %shard_map.73 = f32[2,4,16,2,8,128]{5,4,3,2,1,0:T(8,128)} custom-call(f32[2,2,1024,128]{3,2,1,0:T(8,128)} %bitcast.11, f32[2,8,256,64]{3,2,1,0:T(8,128)} %bitcast.12, f32[64,128]{1,0:T(8,128)} %bitcast.13, f32[8,16]{1,0:T(8,128)} %first_hbm.1, f32[8,16]{1,0:T(8,128)} %second_hbm.1, f32[16,16]{1,0:T(8,128)} %third_hbm.1), custom_call_target="tpu_custom_call" | custom-call | tf_op jit(solution)/shard_map/pallas_call | solution.py:309
  61.0 3.5 %shard_map.74 = f32[2,2,1024,128]{3,2,1,0:T(8,128)} custom-call(f32[128,2,8,128]{3,2,1,0:T(8,128)} %bitcast.10, f32[64,128]{1,0:T(8,128)} %bitcast.14), custom_call_target="tpu_custom_call" | custom-call | tf_op jit(solution)/shard_map/pallas_call | solution.py:339

commit v4 on v3

--- a/solution.py
+++ b/solution.py
@@ -74,7 +74,7 @@
     def hops(d):
         return (0, 1, 2, 1)[d // 8] + (d // 4) % 2 + (0, 1, 2, 1)[d % 4]
 
-    for d in sorted(range(1, 32), key=lambda d: -hops(d)):
+    for d in sorted([d for d in range(1, 32) if d // 4 % 2 == 0 or d == 4], key=lambda d: -hops(d)):
         pl.semaphore_signal(barrier, inc=1, device_id=plane(d - 1), device_id_type=MESH)
     for d in (4, 5, 6, 7, 3, 1):
         pl.semaphore_signal(barrier, inc=1, device_id=square(d - 1), device_id_type=MESH)
@@ -141,7 +141,7 @@
 
     third_step(0)
     project(0)
-    pl.semaphore_wait(barrier, 37)
+    pl.semaphore_wait(barrier, 22)
     swap(0).start()
     send_b(0)
     third_step(1)
@@ -285,17 +285,33 @@
     pltpu.make_async_copy(ys.at[:, 0:31], ys.at[:, 0:31], y_send).wait()
 
 
-def finish_kernel(modes_ref, fout_ref, out_ref):
+def finish_kernel(modes_hbm, fout_hbm, out_hbm, modes_ref, fout_ref, out_ref, in_sem, out_sem):
+    load_factor = pltpu.make_async_copy(fout_hbm, fout_ref, in_sem.at[2])
+    loads = [
+        pltpu.make_async_copy(modes_hbm.at[:, b], modes_ref.at[b], in_sem.at[b]) for b in range(2)
+    ]
+    load_factor.start()
+    for load in loads:
+        load.start()
+    load_factor.wait()
     factor = fout_ref[...].T
     blank = jnp.zeros_like(factor)
     wide = jnp.concatenate(
         [jnp.concatenate([factor, blank], axis=1), jnp.concatenate([blank, factor], axis=1)], axis=0
     )
-    modes = modes_ref.reshape(1024, 128)
-    for k in range(8):
-        mixed = dot(wide, modes[pl.ds(k, 128, stride=8), :], ((1,), (1,)))
-        out_ref[0, 0, pl.ds(k, 128, stride=8), :] = mixed[0:128]
-        out_ref[1, 0, pl.ds(k, 128, stride=8), :] = mixed[128:256]
+    stores = []
+    for b in range(2):
+        loads[b].wait()
+        modes = modes_ref.at[b].reshape(1024, 128)
+        for k in range(8):
+            mixed = dot(wide, modes[pl.ds(k, 128, stride=8), :], ((1,), (1,)))
+            out_ref[0, b, pl.ds(k, 128, stride=8), :] = mixed[0:128]
+            out_ref[1, b, pl.ds(k, 128, stride=8), :] = mixed[128:256]
+        store = pltpu.make_async_copy(out_ref.at[:, b], out_hbm.at[:, b], out_sem.at[b])
+        store.start()
+        stores.append(store)
+    for store in stores:
+        store.wait()
 
 
 def per_device(
@@ -338,13 +354,12 @@
     )(spec, core, input_factor.T, first_factor, second_factor, third_factor)
     out = pl.pallas_call(
         finish_kernel,
-        grid=(2,),
         out_shape=jax.ShapeDtypeStruct((2, 2, 1024, 128), F32),
-        in_specs=[
-            pl.BlockSpec((128, 1, 8, 128), lambda b: (0, b, 0, 0)),
-            pl.BlockSpec((64, 128), lambda b: (0, 0)),
+        in_specs=[anywhere, anywhere],
+        out_specs=anywhere,
+        scratch_shapes=[
+            vmem(2, 128, 8, 128), vmem(64, 128), vmem(2, 2, 1024, 128), dma((3,)), dma((2,)),
         ],
-        out_specs=pl.BlockSpec((2, 1, 1024, 128), lambda b: (0, b, 0, 0)),
         compiler_params=pltpu.CompilerParams(vmem_limit_bytes=63 * 1024 * 1024),
     )(values.reshape(128, 2, 8, 128), output_factor.T)
     return out.reshape(2, 2, 128, 8, 128)

time: 65.2 us -> 65 us (level)
  no operation moved by 1% of the time
where the time goes in v4:
time: 65 us; the launch traced here: 64.2 us
  Pallas kernels  64.2 us (99%)
    pallas_call x1, Pallas kernels, per_device(): pl.pallas_call(kernel, out_shape=jax.ShapeDtypeStruct((2, 4, 16, 2, 8, 12...  61 us
    pallas_call x1, Pallas kernels, per_device(): pl.pallas_call(finish_kernel, out_shape=jax.ShapeDtypeStruct((2, 2, 1024,...  3.26 us

profile of v4, /device:TPU:1, one launch (start us, length us, event | category | flops | bytes accessed | tf_op | source)
XLA Modules:
  0.0 64.2 jit_solution(12006148603384311507)
XLA Ops:
  0.0 61.0 %shard_map.73 = f32[2,4,16,2,8,128]{5,4,3,2,1,0:T(8,128)} custom-call(f32[2,2,1024,128]{3,2,1,0:T(8,128)} %bitcast.11, f32[2,8,256,64]{3,2,1,0:T(8,128)} %bitcast.12, f32[64,128]{1,0:T(8,128)} %bitcast.13, f32[8,16]{1,0:T(8,128)} %first_hbm.1, f32[8,16]{1,0:T(8,128)} %second_hbm.1, f32[16,16]{1,0:T(8,128)} %third_hbm.1), custom_call_target="tpu_custom_call" | custom-call | tf_op jit(solution)/shard_map/pallas_call | solution.py:325
  61.0 3.3 %shard_map.74 = f32[2,2,1024,128]{3,2,1,0:T(8,128)} custom-call(f32[128,2,8,128]{3,2,1,0:T(8,128)} %bitcast.10, f32[64,128]{1,0:T(8,128)} %bitcast.14), custom_call_target="tpu_custom_call" | custom-call | tf_op jit(solution)/shard_map/pallas_call | solution.py:355

commit v5 on v4

--- a/solution.py
+++ b/solution.py
@@ -199,18 +199,17 @@
 
         lax.fori_loop(0, 2, second_step, 0)
 
-        def send_c(n, carry, half=half):
-            j, i = n // 7, n % 7
-            tz, tmy, tcol = square(i)
-            pltpu.make_async_remote_copy(
-                cs.at[half, tmy * 2 + tcol // 4, j],
-                cr.at[j, my, l, half],
-                c_send, c_recv.at[j],
-                device_id=(tz, tmy, tcol), device_id_type=MESH,
-            ).start()
-            return carry
-
-        lax.fori_loop(0, 28, send_c, 0)
+        def send_c(j, carry, half=half):
+            for d in (2, 3, 4, 5, 6, 7, 1):
+                tz, tmy, tcol = square(d - 1)
+                pltpu.make_async_remote_copy(
+                    cs.at[half, tmy * 2 + lax.div(tcol, 4), j], cr.at[j, my, l, half],
+                    c_send, c_recv.at[j],
+                    device_id=(tz, tmy, tcol), device_id_type=MESH,
+                ).start()
+            return carry
+
+        lax.fori_loop(0, 4, send_c, 0)
 
         def keep_c(n, carry, half=half):
             j, zs = n // 4, n % 4

time: 65 us -> 64.9 us (level)
  no operation moved by 1% of the time
where the time goes in v5:
time: 64.9 us; the launch traced here: 64.1 us
  Pallas kernels  64.1 us (99%)
    pallas_call x1, Pallas kernels, per_device(): pl.pallas_call(kernel, out_shape=jax.ShapeDtypeStruct((2, 4, 16, 2, 8, 12...  60.8 us
    pallas_call x1, Pallas kernels, per_device(): pl.pallas_call(finish_kernel, out_shape=jax.ShapeDtypeStruct((2, 2, 1024,...  3.26 us

profile of v5, /device:TPU:1, one launch (start us, length us, event | category | flops | bytes accessed | tf_op | source)
XLA Modules:
  0.0 64.1 jit_solution(11174267335912140509)
XLA Ops:
  0.0 60.8 %shard_map.73 = f32[2,4,16,2,8,128]{5,4,3,2,1,0:T(8,128)} custom-call(f32[2,2,1024,128]{3,2,1,0:T(8,128)} %bitcast.11, f32[2,8,256,64]{3,2,1,0:T(8,128)} %bitcast.12, f32[64,128]{1,0:T(8,128)} %bitcast.13, f32[8,16]{1,0:T(8,128)} %first_hbm.1, f32[8,16]{1,0:T(8,128)} %second_hbm.1, f32[16,16]{1,0:T(8,128)} %third_hbm.1), custom_call_target="tpu_custom_call" | custom-call | tf_op jit(solution)/shard_map/pallas_call | solution.py:324
  60.8 3.3 %shard_map.74 = f32[2,2,1024,128]{3,2,1,0:T(8,128)} custom-call(f32[128,2,8,128]{3,2,1,0:T(8,128)} %bitcast.10, f32[64,128]{1,0:T(8,128)} %bitcast.14), custom_call_target="tpu_custom_call" | custom-call | tf_op jit(solution)/shard_map/pallas_call | solution.py:354

commit v6 on v5

--- a/solution.py
+++ b/solution.py
@@ -231,45 +231,42 @@
 
     def mode_step(j, carry):
         pltpu.make_async_copy(cs.at[:, 0:7, 0], cs.at[:, 0:7, 0], c_recv.at[j]).wait()
-        high, low = split(xr[:, j].reshape(512, 128))
-        both = jnp.concatenate([high, low], axis=1)
-
-        def group(g):
+        weights = []
+        for g in range(4):
             parts = []
             for i in range(4):
                 top = cr[j, i, :, :, g].reshape(64, 128)
                 parts.append(jnp.concatenate([top, pltpu.roll(top, 64, 1) * sign], axis=0))
             upper, lower = split(jnp.concatenate(parts, axis=1))
-            twice = jnp.concatenate([upper, upper], axis=0)
-            one = lambda u, v: lax.dot_general(
-                u, v, (((1,), (0,)), ((), ())), preferred_element_type=F32
-            )
-            prod = one(both, twice) + one(high, lower)
-            total = None
-            for i in range(4):
-                piece = prod[:, i * 128 : (i + 1) * 128].reshape(2, 4, 8, 8, 128)
-                term = piece * coef[g * 4 + i].reshape(1, 4, 1, 8, 128)
-                total = term if total is None else total + term
-            return total.reshape(2, 32, 8, 128)
-
-        for g in range(4):
-            total = group(g)
-            for b in range(2):
+            weights.append((jnp.concatenate([upper, upper], axis=0), lower))
+        one = lambda u, v: lax.dot_general(
+            u, v, (((1,), (0,)), ((), ())), preferred_element_type=F32
+        )
+        for b in range(2):
+            high, low = split(xr[b, j].reshape(256, 128))
+            both = jnp.concatenate([high, low], axis=1)
+            for g in range(4):
+                prod = one(both, weights[g][0]) + one(high, weights[g][1])
+                total = None
+                for i in range(4):
+                    piece = prod[:, i * 128 : (i + 1) * 128].reshape(4, 8, 8, 128)
+                    term = piece * coef[g * 4 + i].reshape(4, 1, 8, 128)
+                    total = term if total is None else total + term
                 if g == 0:
-                    ys[j, :, b] = total[b]
+                    ys[j, :, b] = total.reshape(32, 8, 128)
                 else:
-                    ys[j, :, b] += total[b]
-
-        def send_y(i, inner):
-            d = jnp.where(i < 16, (i // 4) * 8 + 4 + i % 4, ((i - 15) // 4) * 8 + (i - 15) % 4)
-            tz, tmy, tcol = plane(d - 1)
-            pltpu.make_async_remote_copy(
-                ys.at[j, tz * 8 + tcol], yr.at[l, j, kz], y_send, y_recv,
-                device_id=(tz, tmy, tcol), device_id_type=MESH,
-            ).start()
-            return inner
-
-        lax.fori_loop(0, 31, send_y, 0)
+                    ys[j, :, b] += total.reshape(32, 8, 128)
+
+            def send_y(i, inner, b=b):
+                d = jnp.where(i < 16, (i // 4) * 8 + 4 + i % 4, ((i - 15) // 4) * 8 + (i - 15) % 4)
+                tz, tmy, tcol = plane(d - 1)
+                pltpu.make_async_remote_copy(
+                    ys.at[j, tz * 8 + tcol, b], yr.at[l, j, kz, b], y_send, y_recv,
+                    device_id=(tz, tmy, tcol), device_id_type=MESH,
+                ).start()
+                return inner
+
+            lax.fori_loop(0, 31, send_y, 0)
         pltpu.make_async_copy(ys.at[j, z * 8 + col], yr.at[l, j, kz], y_own).start()
         return carry
 

time: 64.9 us -> 65.1 us (level)
  no operation moved by 1% of the time
where the time goes in v6:
time: 65.1 us; the launch traced here: 64.7 us
  Pallas kernels  64.7 us (99%)
    pallas_call x1, Pallas kernels, per_device(): pl.pallas_call(kernel, out_shape=jax.ShapeDtypeStruct((2, 4, 16, 2, 8, 12...  61.4 us
    pallas_call x1, Pallas kernels, per_device(): pl.pallas_call(finish_kernel, out_shape=jax.ShapeDtypeStruct((2, 2, 1024,...  3.26 us

profile of v6, /device:TPU:1, one launch (start us, length us, event | category | flops | bytes accessed | tf_op | source)
XLA Modules:
  0.0 64.7 jit_solution(15249343586217700901)
XLA Ops:
  0.0 61.4 %shard_map.73 = f32[2,4,16,2,8,128]{5,4,3,2,1,0:T(8,128)} custom-call(f32[2,2,1024,128]{3,2,1,0:T(8,128)} %bitcast.11, f32[2,8,256,64]{3,2,1,0:T(8,128)} %bitcast.12, f32[64,128]{1,0:T(8,128)} %bitcast.13, f32[8,16]{1,0:T(8,128)} %first_hbm.1, f32[8,16]{1,0:T(8,128)} %second_hbm.1, f32[16,16]{1,0:T(8,128)} %third_hbm.1), custom_call_target="tpu_custom_call" | custom-call | tf_op jit(solution)/shard_map/pallas_call | solution.py:321
  61.4 3.3 %shard_map.74 = f32[2,2,1024,128]{3,2,1,0:T(8,128)} custom-call(f32[128,2,8,128]{3,2,1,0:T(8,128)} %bitcast.10, f32[64,128]{1,0:T(8,128)} %bitcast.14), custom_call_target="tpu_custom_call" | custom-call | tf_op jit(solution)/shard_map/pallas_call | solution.py:351
